TPU v7x, 32 devices: a whole 2x2x4 slice. The times are simulated.
32 devices in a mesh: tm: 4 (over y, core), space: 8 (over z, x).
Axes of the slice: x: 2, y: 2, z: 4, core: 2. Of those that a mesh axis runs over, the one named last changes fastest.
Arguments:
- state: float32 [4, 4, 16, 128, 128], P('tm', None, 'space'), may hold values from -6 to 6
- source: float32 [4, 4, 16, 128, 128], P('tm', None, 'space'), may hold values from -6 to 6
- start_field: float32 [16, 128, 128], P('space'), may hold values from -6 to 6
- diffusion: float32 [16, 128, 128], P('space'), may hold values from 0.1 to 1
- reaction: float32 [16, 128, 128], P('space'), may hold values from 0.3 to 3
- section_matrix: float32 [4, 4], replicated, may hold values from -0.5 to 3.5, as said below
- end_weights: float32 [4], replicated, may hold values from 0.2 to 0.6
Outputs:
- smoothed: float32 [4, 4, 16, 128, 128], P('tm', None, 'space')
Inputs may be any that keep to these rules, and one draw needn't show every extreme that they name: `section_matrix`: diagonal entries lie between 2 and 3.5, the others between -0.5 and 0.5.
All inputs are finite; a program needn't handle non-finite values.
Results may differ from a plain program's by a relative error of at most 0.0001.
Values sent between devices are 32-bit elements; how exact they have to be, the bound alone decides.
No kernel may reach another device: no remote copies, remote signals or barrier semaphores. Data moves between devices by JAX's collectives and lax.ppermute only.
A program may use at most 64 MiB of HBM per device.

v0:
```python
import functools

import jax
import jax.numpy as jnp
from jax import lax
from jax.experimental import pallas as pl
from jax.experimental.pallas import tpu as pltpu
from jax.sharding import PartitionSpec as P


HALO = 8
SUB = 8

VMEM = pl.BlockSpec(memory_space=pltpu.VMEM)
HBM = pl.BlockSpec(memory_space=pltpu.HBM)
F32 = jnp.float32


def permutations(slabs, blocks):
    ys, zs = slabs // 2, blocks // 2

    def at(y, c, z, x):
        return (2 * y + c) * blocks + 2 * z + x

    everyone = [(y, c, z, x) for y in range(ys) for c in range(2) for z in range(zs) for x in range(2)]

    def depth(y, c, z, x, edge):
        if c == 1:
            return at(y, 0, z + 1, x) if z + 1 < zs else edge
        return at(y, 1, z - 1, x) if z > 0 else edge

    maps = {
        "first": lambda y, c, z, x: at(y, x, z, c),
        "second": lambda y, c, z, x: at(y, x, z, 1 - c),
        "back": lambda y, c, z, x: at(y, 1 - x, z, c),
        "depth": lambda y, c, z, x: depth(y, c, z, x, at(y, c, z, 1 - x)),
        "depth_early": lambda y, c, z, x: depth(y, c, z, x, at(y ^ 1 if y ^ 1 < ys else y, c, z, x)),
        "core": lambda y, c, z, x: at(y, 1 - c, z, x),
        "time": lambda y, c, z, x: at((y + 1) % ys, c, z, x),
    }
    return {name: [(at(*d), move(*d)) for d in everyone] for name, move in maps.items()}


def call(body, ins, outs, scratch=()):
    specs = [spec for spec, _ in ins]
    return pl.pallas_call(
        body,
        in_specs=specs,
        out_specs=[spec for spec, _ in outs],
        out_shape=[jax.ShapeDtypeStruct(shape, F32) for _, shape in outs],
        scratch_shapes=list(scratch),
        compiler_params=pltpu.CompilerParams(vmem_limit_bytes=8 << 20),
    )(*[value for _, value in ins])


def run_copies(copies, sems):
    started = [pltpu.make_async_copy(src, dst, sems.at[i]) for i, (src, dst) in enumerate(copies)]
    for copy in started:
        copy.start()
    for copy in started:
        copy.wait()


def place_of():
    return lax.axis_index("tm") % 2, lax.axis_index("space") % 2


def pack_kernel(*refs):
    fields, (first, second, sems) = refs[:-3], refs[-3:]
    core, x = place_of()
    field = fields[0]
    sections, rows = field.shape[1], first.shape[-2]
    step = field.shape[3] - rows
    near = pl.ds(pl.multiple_of(core * step, SUB), rows)
    far = pl.ds(pl.multiple_of((1 - core) * step, SUB), rows)
    copies = []
    for slot, plane in enumerate((x, 1 - x)):
        copies.append((field.at[0, :, plane, near], first.at[slot]))
        copies.append((field.at[0, :, plane, far], second.at[slot, pl.ds(0, sections)]))
        for index, coef in enumerate(fields[1:]):
            copies.append((coef.at[plane, far], second.at[slot, sections + index]))
    run_copies(copies, sems)


def chunks(rows):
    return [(k, pl.ds(k * SUB, SUB)) for k in range(rows // SUB)]


class Table:
    def __init__(self, ref, sections):
        self.ref, self.sections = ref, sections

    def matrix(self, s, r):
        return self.ref[s * self.sections + r]

    def weight(self, r):
        return self.ref[self.sections * self.sections + r]

    def mask(self, index):
        return self.ref[self.sections * (self.sections + 1) + index]

    def off_mix(self, s, values):
        return sum(self.matrix(s, r) * values[r] for r in range(self.sections) if r != s)

    def weighted(self, values):
        return sum(self.weight(r) * value for r, value in enumerate(values))


CONTINUES, INSIDE, LEFT = range(3)


def table_of(matrix, weights):
    tm, space = lax.axis_index("tm"), lax.axis_index("space")
    depth, x = space // 2, space % 2
    edge = jnp.where(tm % 2 == 0, 0, lax.axis_size("space") // 2 - 1)
    masks = jnp.stack([tm // 2 != 0, depth != edge, x == 0]).astype(F32)
    flat = jnp.concatenate([matrix.reshape(-1), weights, masks])
    return jnp.broadcast_to(flat[:, None, None], (flat.shape[0], SUB, 128))


def order_kernel(table, first, second, outer, inner, ends):
    sections = outer.shape[1]
    params = Table(table, sections)
    left = params.mask(LEFT) > 0.5
    for slot, field in enumerate((outer, inner)):
        for _, rows in chunks(field.shape[2]):
            later = []
            for s in range(sections):
                a, b = first[slot, s, rows], second[slot, s, rows]
                field[0, s, rows] = jnp.where(left, a, b)
                later.append(jnp.where(left, b, a))
                field[1, s, rows] = later[-1]
            ends[slot, rows] = params.weighted(later)


def put_ends(refs, rows, ends, slot):
    if slot == 0:
        refs[-1][0, rows] = ends
        refs[-1][1, rows] = refs[0][rows]
    else:
        refs[-1][rows] = ends


def scale_kernel(table, first, second, *outs):
    sections = first.shape[1]
    params = Table(table, sections)
    left = params.mask(LEFT) > 0.5
    begins = 1.0 - params.mask(CONTINUES)
    for slot in range(2):
        source, coefs, fine, coarse = outs[4 * slot : 4 * slot + 4]
        for _, rows in chunks(first.shape[2]):
            for s in range(sections):
                a, b = first[slot, s, rows], second[slot, s, rows]
                source[0, s, rows] = jnp.where(left, a, b)
                source[1, s, rows] = jnp.where(left, b, a)
            diffusion, reaction = second[slot, sections, rows], second[slot, sections + 1, rows]
            coefs[0, rows] = diffusion
            coefs[1, rows] = reaction
            coefs[2, rows] = begins * second[slot, sections + 2, rows]
            base = 6.0 * diffusion + reaction
            for s in range(sections):
                fine[s, rows] = 1.0 / (params.matrix(s, s) + base)
                coarse[s, rows] = 1.0 / (params.matrix(s, s) + 2.0 * base)


def edges():
    lane = lax.broadcasted_iota(jnp.int32, (SUB, 128), 1)
    row = lax.broadcasted_iota(jnp.int32, (SUB, 128), 0)
    return lane == 0, lane == 127, row == 0, row == SUB - 1


def around(read, total, k, center, masks):
    left, right, top, bottom = masks
    lanes = center.shape[1]
    near = jnp.where(left, 0.0, pltpu.roll(center, 1, 1)) + jnp.where(right, 0.0, pltpu.roll(center, lanes - 1, 1))
    if k == 0:
        above = jnp.where(top, 0.0, pltpu.roll(center, 1, 0))
    else:
        above = read(pl.ds(k * SUB - 1, SUB))
    if k == total - 1:
        below = jnp.where(bottom, 0.0, pltpu.roll(center, SUB - 1, 0))
    else:
        below = read(pl.ds(k * SUB + 1, SUB))
    return near + (above + below)


def fine_kernel(table, field, other, halo, arrived, source, coefs, scale, *refs, slot, weight, last, sums=False, parts=False):
    total = field.shape[2] // SUB
    sections = field.shape[1]
    params = Table(table, sections)
    masks = edges()
    left = params.mask(LEFT) > 0.5
    x = place_of()[1] if last else None
    for k, rows in chunks(field.shape[2]):
        diffusion, reaction = coefs[0, rows], coefs[1, rows]
        values = [[field[n, s, rows] for s in range(sections)] for n in range(2)]
        befores = [coefs[2, rows] + params.mask(CONTINUES) * arrived[slot, rows], params.weighted(values[0])]
        updated = []
        for n in range(2):
            for s in range(sections):
                value = values[n][s]
                if slot == 1 or not parts:
                    beside = halo[n, s, rows]
                elif n == 0:
                    beside = refs[1][s, rows] + halo[s, rows]
                else:
                    beside = refs[2][s, rows] - refs[1][s, rows] + halo[s, rows]
                if slot == 0:
                    beside = beside * params.mask(INSIDE)
                near = around(lambda at, n=n, s=s: field[n, s, at], total, k, value, masks)
                near = near + (other[n, s, rows] + beside)
                acc = (source[n, s, rows] + befores[n]) + diffusion * near
                acc = acc - params.off_mix(s, values[n]) - reaction * (jnp.tanh(value) - value)
                new = scale[s, rows] * acc
                if weight != 1.0:
                    new = (1.0 - weight) * value + weight * new
                updated.append(new)
        if not last:
            out = refs[-4 if sums and slot == 0 else -2]
            for n in range(2):
                for s in range(sections):
                    out[n, s, rows] = updated[n * sections + s]
            if sums and slot == 0:
                for s in range(sections):
                    refs[-3][s, rows] = updated[s] + updated[sections + s]
                    refs[-2][s, rows] = updated[s]
            put_ends(refs, rows, params.weighted(updated[sections:]), slot)
        else:

            def put(k=k, updated=updated):
                place = pl.ds(pl.multiple_of((k - x) * SUB, SUB), SUB)
                for s in range(sections):
                    a, b = updated[s], updated[sections + s]
                    refs[0][s, place] = jnp.where(left, a, b)
                    refs[1][s, place] = jnp.where(left, b, a)

            if k == 0:
                pl.when(x == 0)(put)
            elif k == total - 1:
                pl.when(x == 1)(put)
            else:
                put()


def residual_kernel(table, field, other, halo, arrived, source, coefs, scale, *refs, slot):
    total = field.shape[2] // SUB
    sections = field.shape[1]
    params = Table(table, sections)
    masks = edges()
    kept, out = refs[-3], refs[-2]
    for k, rows in chunks(field.shape[2]):
        diffusion, reaction = coefs[0, rows], coefs[1, rows]
        firsts = [field[0, s, rows] for s in range(sections)]
        seconds = [field[1, s, rows] for s in range(sections)]
        both = [a + b for a, b in zip(firsts, seconds)]
        before = coefs[2, rows] + params.mask(CONTINUES) * arrived[slot, rows] + params.weighted(firsts)
        made = []
        for s in range(sections):
            if slot == 0:
                beside = halo[s, rows] * params.mask(INSIDE)
            else:
                beside = halo[0, s, rows] + halo[1, s, rows]
            near = around(lambda at, s=s: field[0, s, at] + field[1, s, at], total, k, both[s], masks)
            near = near + (other[0, s, rows] + other[1, s, rows] + beside)
            acc = (source[0, s, rows] + source[1, s, rows]) + before + diffusion * (near - 6.0 * both[s])
            acc = acc - (params.off_mix(s, both) + params.matrix(s, s) * both[s])
            acc = acc - reaction * (jnp.tanh(firsts[s]) + jnp.tanh(seconds[s]))
            kept[s, rows] = acc
            new = 0.7 * (acc * scale[s, rows])
            out[s, rows] = new
            made.append(new)
        put_ends(refs, rows, params.weighted(made), slot)


def coarse_kernel(table, field, other, halo, arrived, source, coefs, scale, *refs, slot, weight, last):
    total = field.shape[1] // SUB
    sections = field.shape[0]
    params = Table(table, sections)
    masks = edges()
    out = refs[-2]
    for k, rows in chunks(field.shape[1]):
        double = 2.0 * coefs[0, rows]
        values = [field[s, rows] for s in range(sections)]
        before = params.mask(CONTINUES) * arrived[slot, rows]
        made = []
        for s in range(sections):
            beside = halo[s, rows]
            if slot == 0:
                beside = beside * params.mask(INSIDE)
            near = around(lambda at, s=s: field[s, at], total, k, values[s], masks)
            near = near + (other[s, rows] + beside)
            acc = (source[s, rows] + before) + double * near - params.off_mix(s, values)
            new = scale[s, rows] * acc
            if weight != 1.0:
                new = (1.0 - weight) * values[s] + weight * new
            made.append(new)
        if last:
            fine = refs[-4 if slot == 0 else -3]
            if slot == 0:
                out = refs[-3]
                for s in range(sections):
                    refs[-2][s, rows] = made[s]
            for n in range(2):
                for s in range(sections):
                    out[n, s, rows] = fine[n, s, rows] + made[s]
            made = [fine[1, s, rows] + made[s] for s in range(sections)]
        else:
            for s in range(sections):
                out[s, rows] = made[s]
        put_ends(refs, rows, params.weighted(made), slot)


def place_kernel(first_outer, second_outer, first_inner, second_inner, out, sems):
    core, x = place_of()
    half = first_outer.shape[1]
    copies = []
    for plane, parts in ((x, (first_outer, second_outer)), (1 - x, (first_inner, second_inner))):
        for part, which in zip(parts, (core, 1 - core)):
            start = pl.multiple_of(which * half, SUB)
            copies.append((part, out.at[0, :, plane, pl.ds(start, half)]))
    run_copies(copies, sems)


def local(state, source, start_field, diffusion, reaction, matrix, weights, moves):
    sections, ny, nz = state.shape[1], state.shape[3], state.shape[4]
    half = ny // 2
    rows = half + HALO
    plane, pair = (sections, rows, nz), (2, sections, rows, nz)
    single, double = (rows, nz), (2, rows, nz)

    def move(value, name):
        return lax.ppermute(value, ("tm", "space"), moves[name])

    def within(*values):
        return [(VMEM, v) for v in values]

    def pack(fields):
        first, second = call(
            pack_kernel,
            [(HBM, pltpu.with_memory_space_constraint(v, pltpu.HBM)) for v in fields],
            within(pair, (2, sections + len(fields) - 1, rows, nz)),
            [pltpu.SemaphoreType.DMA((2 * len(fields) + 2,))],
        )
        return move(first, "first"), move(second, "second")

    states = pack((state,))
    given = pack((source, diffusion, reaction, start_field))
    table = table_of(matrix, weights)
    outer, inner, ends = call(order_kernel, within(table, *states), within(pair, pair, double))
    kept = call(scale_kernel, within(table, *given), within(pair, (3, rows, nz), plane, plane) * 2)
    sources, coefs, fines, coarses = zip(kept[:4], kept[4:])

    def exchange(sent, inner, ends, name):
        depth = move(sent, "depth_early" if name == "fine_0" else "depth")
        arrived = move(ends, "time")
        return depth, move(inner, "core"), arrived

    def step(body, fields, sent, ends, source, scale, outs, name, extra=((), ()), more_outs=()):
        outer, inner = fields
        depth, beside, arrived = exchange(sent, inner, ends, name)
        halos[name] = depth

        def half_step(slot, own, other, halo, *more):
            return call(
                functools.partial(body, slot=slot),
                within(table, own, other, halo, arrived, source[slot], coefs[slot], scale[slot], *more, *extra[slot]),
                within(*outs, *(more_outs if slot == 0 else ()), single if slot else double),
            )

        made = half_step(1, inner, outer, beside)
        made_o = half_step(0, outer, inner, depth, made[-1])
        return list(zip(made_o, made[:-1])), made_o[len(outs) : -1], made_o[-1]

    def fine(weight, **options):
        return functools.partial(fine_kernel, weight=weight, last=False, **options)

    halos = {}
    fields = (outer, inner)
    (fields,), _, ends = step(fine(0.6), fields, outer, ends, sources, fines, [pair], "fine_0")
    (fields,), (both, first), ends = step(
        fine(1.0, sums=True), fields, fields[0], ends, sources, fines, [pair], "fine_1", more_outs=(plane, plane)
    )
    (kept, coarse), _, ends = step(residual_kernel, fields, both, ends, sources, coarses, [plane, plane], "residual")
    first, both = move(first, "depth"), halos["residual"]
    body = functools.partial(coarse_kernel, weight=1.0, last=False)
    (coarse,), _, ends = step(body, coarse, coarse[0], ends, kept, coarses, [plane], "coarse")
    body = functools.partial(coarse_kernel, weight=0.7, last=True)
    (fields,), (change,), ends = step(
        body, coarse, coarse[0], ends, kept, coarses, [pair], "correct", extra=[(f,) for f in fields], more_outs=(plane,)
    )
    (fields,), _, ends = step(
        fine(1.0, parts=True), fields, change, ends, sources, fines, [pair], "fine_2", extra=((first, both), ())
    )
    outer, inner = fields

    depth, beside, arrived = exchange(outer, inner, ends, "last")
    body = functools.partial(fine_kernel, weight=0.6, last=True)
    parts = []
    for slot, own, other, halo in ((1, inner, outer, beside), (0, outer, inner, depth)):
        first, second = call(
            functools.partial(body, slot=slot),
            within(table, own, other, halo, arrived, sources[slot], coefs[slot], fines[slot]),
            within(*[(sections, half, nz)] * 2),
        )
        parts.append((move(first, "first"), move(second, "back")))
    (out,) = call(place_kernel, within(*parts[1], *parts[0]), [(HBM, state.shape)], [pltpu.SemaphoreType.DMA((4,))])
    return out


def solution(mesh):
    moves = permutations(mesh.shape["tm"], mesh.shape["space"])
    in_specs = (
        P("tm", None, "space", None, None),
        P("tm", None, "space", None, None),
        P("space", None, None),
        P("space", None, None),
        P("space", None, None),
        P(),
        P(),
    )
    out_specs = P("tm", None, "space", None, None)

    def body(*args):
        return local(*args, moves=moves)

    return jax.shard_map(body, mesh=mesh, in_specs=in_specs, out_specs=out_specs, check_vma=False)
```

profile of v0, /device:TPU:0, one launch (start us, length us, event | category | flops | bytes accessed | tf_op | source)
XLA Modules:
  0.0 78.1 jit_solution(9537656308874697441)
XLA Ops:
  1.9 4.2 %collective-permute-start.1 = (f32[2,4,72,128]{3,2,1,0:T(8,128)S(1)}, f32[2,4,72,128]{3,2,1,0:T(8,128)S(1)}, u32[]{:S(2)}, u32[]{:S(2)}) collective-permute-start(f32[2,4,72,128]{3,2,1,0:T(8,128)S(1)} %get-tuple-element.54), channel_id=1, source_target_pairs={{0,1},{1,9},{2,3},{3,11},{4,5},{5,13},{6,7},{7,15},{8,0},{9,8},{10... | collective-permute-start | bytes 884744 | tf_op jit(solution)/shard_map/ppermute | solution.py:332
  9.6 3.8 %collective-permute-done.1.second = f32[2,4,72,128]{3,2,1,0:T(8,128)S(1)} collective-permute-done((f32[2,4,72,128]{3,2,1,0:T(8,128)S(1)}, f32[2,4,72,128]{3,2,1,0:T(8,128)S(1)}, u32[]{:S(2)}, u32[]{:S(2)}) %collective-permute-start.1) | collective-permute-done | bytes 294944 | tf_op jit(solution)/shard_map/ppermute | solution.py:332
  14.9 1.5 %collective-permute-start.2 = (f32[2,4,72,128]{3,2,1,0:T(8,128)S(1)}, f32[2,4,72,128]{3,2,1,0:T(8,128)S(1)}, u32[]{:S(2)}, u32[]{:S(2)}) collective-permute-start(f32[2,4,72,128]{3,2,1,0:T(8,128)S(1)} %get-tuple-element.55.other.field), channel_id=1, source_target_pairs={{0,16},{1,17},{2,8},{3,9},{4,10},{5,11},{6,12},{7,13},{8,2},{9,3},... | collective-permute-start | bytes 884744 | tf_op jit(solution)/shard_map/ppermute | solution.py:332
  16.9 4.6 %collective-permute-done.5.second = f32[2,7,72,128]{3,2,1,0:T(8,128)S(1)} collective-permute-done((f32[2,7,72,128]{3,2,1,0:T(8,128)S(1)}, f32[2,7,72,128]{3,2,1,0:T(8,128)S(1)}, u32[]{:S(2)}, u32[]{:S(2)}) %collective-permute-start.5) | collective-permute-done | bytes 516128 | tf_op jit(solution)/shard_map/ppermute | solution.py:332
  21.7 1.5 %collective-permute-done.3.arrived = f32[2,72,128]{2,1,0:T(8,128)S(1)} collective-permute-done((f32[2,72,128]{2,1,0:T(8,128)S(1)}, f32[2,72,128]{2,1,0:T(8,128)S(1)}, u32[]{:S(2)}, u32[]{:S(2)}) %collective-permute-start.3) | collective-permute-done | bytes 73760 | tf_op jit(solution)/shard_map/ppermute | solution.py:332
  25.4 1.5 %collective-permute-start.8 = (f32[2,72,128]{2,1,0:T(8,128)S(1)}, f32[2,72,128]{2,1,0:T(8,128)S(1)}, u32[]{:S(2)}, u32[]{:S(2)}) collective-permute-start(f32[2,72,128]{2,1,0:T(8,128)S(1)} %get-tuple-element.69), channel_id=1, source_target_pairs={{0,16},{1,17},{2,18},{3,19},{4,20},{5,21},{6,22},{7,23},{8,24},{9,... | collective-permute-start | bytes 221192 | tf_op jit(solution)/shard_map/ppermute | solution.py:332
  26.9 2.8 %collective-permute-done.8.arrived = f32[2,72,128]{2,1,0:T(8,128)S(1)} collective-permute-done((f32[2,72,128]{2,1,0:T(8,128)S(1)}, f32[2,72,128]{2,1,0:T(8,128)S(1)}, u32[]{:S(2)}, u32[]{:S(2)}) %collective-permute-start.8) | collective-permute-done | bytes 73760 | tf_op jit(solution)/shard_map/ppermute | solution.py:332
  31.1 1.4 %collective-permute-start.10 = (f32[4,72,128]{2,1,0:T(8,128)S(1)}, f32[4,72,128]{2,1,0:T(8,128)S(1)}, u32[]{:S(2)}, u32[]{:S(2)}) collective-permute-start(f32[4,72,128]{2,1,0:T(8,128)S(1)} %get-tuple-element.73), channel_id=1, source_target_pairs={{0,1},{1,0},{2,8},{3,9},{4,10},{5,11},{6,12},{7,13},{8,2},{9,3},{1... | collective-permute-start | bytes 442376 | tf_op jit(solution)/shard_map/ppermute | solution.py:332
  32.5 1.5 %collective-permute-start.11 = (f32[2,72,128]{2,1,0:T(8,128)S(1)}, f32[2,72,128]{2,1,0:T(8,128)S(1)}, u32[]{:S(2)}, u32[]{:S(2)}) collective-permute-start(f32[2,72,128]{2,1,0:T(8,128)S(1)} %get-tuple-element.74), channel_id=1, source_target_pairs={{0,16},{1,17},{2,18},{3,19},{4,20},{5,21},{6,22},{7,23},{8,24},{9,... | collective-permute-start | bytes 221192 | tf_op jit(solution)/shard_map/ppermute | solution.py:332
  34.0 2.8 %collective-permute-done.11.arrived = f32[2,72,128]{2,1,0:T(8,128)S(1)} collective-permute-done((f32[2,72,128]{2,1,0:T(8,128)S(1)}, f32[2,72,128]{2,1,0:T(8,128)S(1)}, u32[]{:S(2)}, u32[]{:S(2)}) %collective-permute-start.11) | collective-permute-done | bytes 73760 | tf_op jit(solution)/shard_map/ppermute | solution.py:332
  38.2 1.5 %collective-permute-start.14 = (f32[2,72,128]{2,1,0:T(8,128)S(1)}, f32[2,72,128]{2,1,0:T(8,128)S(1)}, u32[]{:S(2)}, u32[]{:S(2)}) collective-permute-start(f32[2,72,128]{2,1,0:T(8,128)S(1)} %get-tuple-element.80), channel_id=1, source_target_pairs={{0,16},{1,17},{2,18},{3,19},{4,20},{5,21},{6,22},{7,23},{8,24},{9,... | collective-permute-start | bytes 221192 | tf_op jit(solution)/shard_map/ppermute | solution.py:332
  39.8 2.8 %collective-permute-done.14.arrived = f32[2,72,128]{2,1,0:T(8,128)S(1)} collective-permute-done((f32[2,72,128]{2,1,0:T(8,128)S(1)}, f32[2,72,128]{2,1,0:T(8,128)S(1)}, u32[]{:S(2)}, u32[]{:S(2)}) %collective-permute-start.14) | collective-permute-done | bytes 73760 | tf_op jit(solution)/shard_map/ppermute | solution.py:332
  43.0 1.6 %collective-permute-start.17 = (f32[2,72,128]{2,1,0:T(8,128)S(1)}, f32[2,72,128]{2,1,0:T(8,128)S(1)}, u32[]{:S(2)}, u32[]{:S(2)}) collective-permute-start(f32[2,72,128]{2,1,0:T(8,128)S(1)} %get-tuple-element.86), channel_id=1, source_target_pairs={{0,16},{1,17},{2,18},{3,19},{4,20},{5,21},{6,22},{7,23},{8,24},{9,... | collective-permute-start | bytes 221192 | tf_op jit(solution)/shard_map/ppermute | solution.py:332
  44.6 3.1 %collective-permute-done.17.arrived = f32[2,72,128]{2,1,0:T(8,128)S(1)} collective-permute-done((f32[2,72,128]{2,1,0:T(8,128)S(1)}, f32[2,72,128]{2,1,0:T(8,128)S(1)}, u32[]{:S(2)}, u32[]{:S(2)}) %collective-permute-start.17) | collective-permute-done | bytes 73760 | tf_op jit(solution)/shard_map/ppermute | solution.py:332
  48.1 1.5 %collective-permute-start.16 = (f32[4,72,128]{2,1,0:T(8,128)S(1)}, f32[4,72,128]{2,1,0:T(8,128)S(1)}, u32[]{:S(2)}, u32[]{:S(2)}) collective-permute-start(f32[4,72,128]{2,1,0:T(8,128)S(1)} %get-tuple-element.84.other.field), channel_id=1, source_target_pairs={{0,1},{1,0},{2,8},{3,9},{4,10},{5,11},{6,12},{7,13},{8,2},{9,3},{1... | collective-permute-start | bytes 442376 | tf_op jit(solution)/shard_map/ppermute | solution.py:332
  50.1 3.1 %collective-permute-done.16.halo = f32[4,72,128]{2,1,0:T(8,128)S(1)} collective-permute-done((f32[4,72,128]{2,1,0:T(8,128)S(1)}, f32[4,72,128]{2,1,0:T(8,128)S(1)}, u32[]{:S(2)}, u32[]{:S(2)}) %collective-permute-start.16) | collective-permute-done | bytes 147488 | tf_op jit(solution)/shard_map/ppermute | solution.py:332
  53.5 1.5 %collective-permute-start.19 = (f32[4,72,128]{2,1,0:T(8,128)S(1)}, f32[4,72,128]{2,1,0:T(8,128)S(1)}, u32[]{:S(2)}, u32[]{:S(2)}) collective-permute-start(f32[4,72,128]{2,1,0:T(8,128)S(1)} %get-tuple-element.90), channel_id=1, source_target_pairs={{0,1},{1,0},{2,8},{3,9},{4,10},{5,11},{6,12},{7,13},{8,2},{9,3},{1... | collective-permute-start | bytes 442376 | tf_op jit(solution)/shard_map/ppermute | solution.py:332
  55.0 1.5 %collective-permute-start.20 = (f32[2,72,128]{2,1,0:T(8,128)S(1)}, f32[2,72,128]{2,1,0:T(8,128)S(1)}, u32[]{:S(2)}, u32[]{:S(2)}) collective-permute-start(f32[2,72,128]{2,1,0:T(8,128)S(1)} %get-tuple-element.91), channel_id=1, source_target_pairs={{0,16},{1,17},{2,18},{3,19},{4,20},{5,21},{6,22},{7,23},{8,24},{9,... | collective-permute-start | bytes 221192 | tf_op jit(solution)/shard_map/ppermute | solution.py:332
  56.5 2.8 %collective-permute-done.20.arrived = f32[2,72,128]{2,1,0:T(8,128)S(1)} collective-permute-done((f32[2,72,128]{2,1,0:T(8,128)S(1)}, f32[2,72,128]{2,1,0:T(8,128)S(1)}, u32[]{:S(2)}, u32[]{:S(2)}) %collective-permute-start.20) | collective-permute-done | bytes 73760 | tf_op jit(solution)/shard_map/ppermute | solution.py:332
  61.0 1.5 %collective-permute-start.24 = (f32[2,72,128]{2,1,0:T(8,128)S(1)}, f32[2,72,128]{2,1,0:T(8,128)S(1)}, u32[]{:S(2)}, u32[]{:S(2)}) collective-permute-start(f32[2,72,128]{2,1,0:T(8,128)S(1)} %get-tuple-element.96), channel_id=1, source_target_pairs={{0,16},{1,17},{2,18},{3,19},{4,20},{5,21},{6,22},{7,23},{8,24},{9,... | collective-permute-start | bytes 221192 | tf_op jit(solution)/shard_map/ppermute | solution.py:332
  62.5 2.8 %collective-permute-done.24.arrived = f32[2,72,128]{2,1,0:T(8,128)S(1)} collective-permute-done((f32[2,72,128]{2,1,0:T(8,128)S(1)}, f32[2,72,128]{2,1,0:T(8,128)S(1)}, u32[]{:S(2)}, u32[]{:S(2)}) %collective-permute-start.24) | collective-permute-done | bytes 73760 | tf_op jit(solution)/shard_map/ppermute | solution.py:332
  66.4 2.6 %collective-permute-start.29 = (f32[4,64,128]{2,1,0:T(8,128)S(1)}, f32[4,64,128]{2,1,0:T(8,128)S(1)}, u32[]{:S(2)}, u32[]{:S(2)}) collective-permute-start(f32[4,64,128]{2,1,0:T(8,128)S(1)} %get-tuple-element.100), channel_id=1, source_target_pairs={{0,8},{1,0},{2,10},{3,2},{4,12},{5,4},{6,14},{7,6},{8,9},{9,1},{10... | collective-permute-start | bytes 393224 | tf_op jit(solution)/shard_map/ppermute | solution.py:332
  71.4 1.8 %collective-permute-done.29.second_inner = f32[4,64,128]{2,1,0:T(8,128)S(1)} collective-permute-done((f32[4,64,128]{2,1,0:T(8,128)S(1)}, f32[4,64,128]{2,1,0:T(8,128)S(1)}, u32[]{:S(2)}, u32[]{:S(2)}) %collective-permute-start.29) | collective-permute-done | bytes 131104 | tf_op jit(solution)/shard_map/ppermute | solution.py:332
  73.2 4.1 %collective-permute-done.26.second_outer = f32[4,64,128]{2,1,0:T(8,128)S(1)} collective-permute-done((f32[4,64,128]{2,1,0:T(8,128)S(1)}, f32[4,64,128]{2,1,0:T(8,128)S(1)}, u32[]{:S(2)}, u32[]{:S(2)}) %collective-permute-start.26) | collective-permute-done | bytes 131104 | tf_op jit(solution)/shard_map/ppermute | solution.py:332
  (63 shorter events, 19.6 us)
Async XLA Ops:
  1.2 8.5 %collective-permute-start = (f32[2,4,72,128]{3,2,1,0:T(8,128)S(1)}, f32[2,4,72,128]{3,2,1,0:T(8,128)S(1)}, u32[]{:S(2)}, u32[]{:S(2)}) collective-permute-start(f32[2,4,72,128]{3,2,1,0:T(8,128)S(1)} %get-tuple-element.53), channel_id=1, source_target_pairs={{0,0},{1,8},{2,2},{3,10},{4,4},{5,12},{6,6},{7,14},{8,1},{9,9},{10... | collective-permute-start | bytes 884744 | tf_op jit(solution)/shard_map/ppermute | solution.py:332
  1.9 11.6 %collective-permute-start.1 = (f32[2,4,72,128]{3,2,1,0:T(8,128)S(1)}, f32[2,4,72,128]{3,2,1,0:T(8,128)S(1)}, u32[]{:S(2)}, u32[]{:S(2)}) collective-permute-start(f32[2,4,72,128]{3,2,1,0:T(8,128)S(1)} %get-tuple-element.54), channel_id=1, source_target_pairs={{0,1},{1,9},{2,3},{3,11},{4,5},{5,13},{6,7},{7,15},{8,0},{9,8},{10... | collective-permute-start | bytes 884744 | tf_op jit(solution)/shard_map/ppermute | solution.py:332
  7.4 14.2 %collective-permute-start.5 = (f32[2,7,72,128]{3,2,1,0:T(8,128)S(1)}, f32[2,7,72,128]{3,2,1,0:T(8,128)S(1)}, u32[]{:S(2)}, u32[]{:S(2)}) collective-permute-start(f32[2,7,72,128]{3,2,1,0:T(8,128)S(1)} %get-tuple-element.59), channel_id=1, source_target_pairs={{0,1},{1,9},{2,3},{3,11},{4,5},{5,13},{6,7},{7,15},{8,0},{9,8},{10... | collective-permute-start | bytes 1548296 | tf_op jit(solution)/shard_map/ppermute | solution.py:332
  7.4 9.5 %collective-permute-start.4 = (f32[2,4,72,128]{3,2,1,0:T(8,128)S(1)}, f32[2,4,72,128]{3,2,1,0:T(8,128)S(1)}, u32[]{:S(2)}, u32[]{:S(2)}) collective-permute-start(f32[2,4,72,128]{3,2,1,0:T(8,128)S(1)} %get-tuple-element.58), channel_id=1, source_target_pairs={{0,0},{1,8},{2,2},{3,10},{4,4},{5,12},{6,6},{7,14},{8,1},{9,9},{10... | collective-permute-start | bytes 884744 | tf_op jit(solution)/shard_map/ppermute | solution.py:332
  13.6 9.6 %collective-permute-start.6 = (f32[2,4,72,128]{3,2,1,0:T(8,128)S(1)}, f32[2,4,72,128]{3,2,1,0:T(8,128)S(1)}, u32[]{:S(2)}, u32[]{:S(2)}) collective-permute-start(f32[2,4,72,128]{3,2,1,0:T(8,128)S(1)} %get-tuple-element.56.field.other), channel_id=1, source_target_pairs={{0,8},{1,9},{2,10},{3,11},{4,12},{5,13},{6,14},{7,15},{8,0},{9,1},... | collective-permute-start | bytes 884744 | tf_op jit(solution)/shard_map/ppermute | solution.py:332
  14.9 8.7 %collective-permute-start.2 = (f32[2,4,72,128]{3,2,1,0:T(8,128)S(1)}, f32[2,4,72,128]{3,2,1,0:T(8,128)S(1)}, u32[]{:S(2)}, u32[]{:S(2)}) collective-permute-start(f32[2,4,72,128]{3,2,1,0:T(8,128)S(1)} %get-tuple-element.55.other.field), channel_id=1, source_target_pairs={{0,16},{1,17},{2,8},{3,9},{4,10},{5,11},{6,12},{7,13},{8,2},{9,3},... | collective-permute-start | bytes 884744 | tf_op jit(solution)/shard_map/ppermute | solution.py:332
  16.4 6.8 %collective-permute-start.3 = (f32[2,72,128]{2,1,0:T(8,128)S(1)}, f32[2,72,128]{2,1,0:T(8,128)S(1)}, u32[]{:S(2)}, u32[]{:S(2)}) collective-permute-start(f32[2,72,128]{2,1,0:T(8,128)S(1)} %get-tuple-element.57), channel_id=1, source_target_pairs={{0,16},{1,17},{2,18},{3,19},{4,20},{5,21},{6,22},{7,23},{8,24},{9,... | collective-permute-start | bytes 221192 | tf_op jit(solution)/shard_map/ppermute | solution.py:332
  23.5 6.2 %collective-permute-start.9 = (f32[2,4,72,128]{3,2,1,0:T(8,128)S(1)}, f32[2,4,72,128]{3,2,1,0:T(8,128)S(1)}, u32[]{:S(2)}, u32[]{:S(2)}) collective-permute-start(f32[2,4,72,128]{3,2,1,0:T(8,128)S(1)} %get-tuple-element.68.field.other), channel_id=1, source_target_pairs={{0,8},{1,9},{2,10},{3,11},{4,12},{5,13},{6,14},{7,15},{8,0},{9,1},... | collective-permute-start | bytes 884744 | tf_op jit(solution)/shard_map/ppermute | solution.py:332
  24.0 6.8 %collective-permute-start.7 = (f32[2,4,72,128]{3,2,1,0:T(8,128)S(1)}, f32[2,4,72,128]{3,2,1,0:T(8,128)S(1)}, u32[]{:S(2)}, u32[]{:S(2)}) collective-permute-start(f32[2,4,72,128]{3,2,1,0:T(8,128)S(1)} %get-tuple-element.67.other.field), channel_id=1, source_target_pairs={{0,1},{1,0},{2,8},{3,9},{4,10},{5,11},{6,12},{7,13},{8,2},{9,3},{1... | collective-permute-start | bytes 884744 | tf_op jit(solution)/shard_map/ppermute | solution.py:332
  30.1 6.8 %collective-permute-start.12 = (f32[2,4,72,128]{3,2,1,0:T(8,128)S(1)}, f32[2,4,72,128]{3,2,1,0:T(8,128)S(1)}, u32[]{:S(2)}, u32[]{:S(2)}) collective-permute-start(f32[2,4,72,128]{3,2,1,0:T(8,128)S(1)} %get-tuple-element.72.field.other.refs_0_), channel_id=1, source_target_pairs={{0,8},{1,9},{2,10},{3,11},{4,12},{5,13},{6,14},{7,15},{8,0},{9,1},... | collective-permute-start | bytes 884744 | tf_op jit(solution)/shard_map/ppermute | solution.py:332
  31.1 6.2 %collective-permute-start.10 = (f32[4,72,128]{2,1,0:T(8,128)S(1)}, f32[4,72,128]{2,1,0:T(8,128)S(1)}, u32[]{:S(2)}, u32[]{:S(2)}) collective-permute-start(f32[4,72,128]{2,1,0:T(8,128)S(1)} %get-tuple-element.73), channel_id=1, source_target_pairs={{0,1},{1,0},{2,8},{3,9},{4,10},{5,11},{6,12},{7,13},{8,2},{9,3},{1... | collective-permute-start | bytes 442376 | tf_op jit(solution)/shard_map/ppermute | solution.py:332
  37.1 5.5 %collective-permute-start.15 = (f32[4,72,128]{2,1,0:T(8,128)S(1)}, f32[4,72,128]{2,1,0:T(8,128)S(1)}, u32[]{:S(2)}, u32[]{:S(2)}) collective-permute-start(f32[4,72,128]{2,1,0:T(8,128)S(1)} %get-tuple-element.79.field.other), channel_id=1, source_target_pairs={{0,8},{1,9},{2,10},{3,11},{4,12},{5,13},{6,14},{7,15},{8,0},{9,1},... | collective-permute-start | bytes 442376 | tf_op jit(solution)/shard_map/ppermute | solution.py:332
  37.5 5.4 %collective-permute-start.13 = (f32[4,72,128]{2,1,0:T(8,128)S(1)}, f32[4,72,128]{2,1,0:T(8,128)S(1)}, u32[]{:S(2)}, u32[]{:S(2)}) collective-permute-start(f32[4,72,128]{2,1,0:T(8,128)S(1)} %get-tuple-element.78.other.field), channel_id=1, source_target_pairs={{0,1},{1,0},{2,8},{3,9},{4,10},{5,11},{6,12},{7,13},{8,2},{9,3},{1... | collective-permute-start | bytes 442376 | tf_op jit(solution)/shard_map/ppermute | solution.py:332
  42.8 5.0 %collective-permute-start.18 = (f32[4,72,128]{2,1,0:T(8,128)S(1)}, f32[4,72,128]{2,1,0:T(8,128)S(1)}, u32[]{:S(2)}, u32[]{:S(2)}) collective-permute-start(f32[4,72,128]{2,1,0:T(8,128)S(1)} %get-tuple-element.85.field.other), channel_id=1, source_target_pairs={{0,8},{1,9},{2,10},{3,11},{4,12},{5,13},{6,14},{7,15},{8,0},{9,1},... | collective-permute-start | bytes 442376 | tf_op jit(solution)/shard_map/ppermute | solution.py:332
  43.0 4.7 %collective-permute-start.17 = (f32[2,72,128]{2,1,0:T(8,128)S(1)}, f32[2,72,128]{2,1,0:T(8,128)S(1)}, u32[]{:S(2)}, u32[]{:S(2)}) collective-permute-start(f32[2,72,128]{2,1,0:T(8,128)S(1)} %get-tuple-element.86), channel_id=1, source_target_pairs={{0,16},{1,17},{2,18},{3,19},{4,20},{5,21},{6,22},{7,23},{8,24},{9,... | collective-permute-start | bytes 221192 | tf_op jit(solution)/shard_map/ppermute | solution.py:332
  48.0 11.3 %collective-permute-start.21 = (f32[2,4,72,128]{3,2,1,0:T(8,128)S(1)}, f32[2,4,72,128]{3,2,1,0:T(8,128)S(1)}, u32[]{:S(2)}, u32[]{:S(2)}) collective-permute-start(f32[2,4,72,128]{3,2,1,0:T(8,128)S(1)} %get-tuple-element.89.field.other), channel_id=1, source_target_pairs={{0,8},{1,9},{2,10},{3,11},{4,12},{5,13},{6,14},{7,15},{8,0},{9,1},... | collective-permute-start | bytes 884744 | tf_op jit(solution)/shard_map/ppermute | solution.py:332
  48.1 5.2 %collective-permute-start.16 = (f32[4,72,128]{2,1,0:T(8,128)S(1)}, f32[4,72,128]{2,1,0:T(8,128)S(1)}, u32[]{:S(2)}, u32[]{:S(2)}) collective-permute-start(f32[4,72,128]{2,1,0:T(8,128)S(1)} %get-tuple-element.84.other.field), channel_id=1, source_target_pairs={{0,1},{1,0},{2,8},{3,9},{4,10},{5,11},{6,12},{7,13},{8,2},{9,3},{1... | collective-permute-start | bytes 442376 | tf_op jit(solution)/shard_map/ppermute | solution.py:332
  49.5 10.2 %collective-permute-start.22 = (f32[4,72,128]{2,1,0:T(8,128)S(1)}, f32[4,72,128]{2,1,0:T(8,128)S(1)}, u32[]{:S(2)}, u32[]{:S(2)}) collective-permute-start(f32[4,72,128]{2,1,0:T(8,128)S(1)} %get-tuple-element.93), channel_id=1, source_target_pairs={{0,1},{1,0},{2,8},{3,9},{4,10},{5,11},{6,12},{7,13},{8,2},{9,3},{1... | collective-permute-start | bytes 442376 | tf_op jit(solution)/shard_map/ppermute | solution.py:332
  53.5 6.2 %collective-permute-start.19 = (f32[4,72,128]{2,1,0:T(8,128)S(1)}, f32[4,72,128]{2,1,0:T(8,128)S(1)}, u32[]{:S(2)}, u32[]{:S(2)}) collective-permute-start(f32[4,72,128]{2,1,0:T(8,128)S(1)} %get-tuple-element.90), channel_id=1, source_target_pairs={{0,1},{1,0},{2,8},{3,9},{4,10},{5,11},{6,12},{7,13},{8,2},{9,3},{1... | collective-permute-start | bytes 442376 | tf_op jit(solution)/shard_map/ppermute | solution.py:332
  59.6 5.7 %collective-permute-start.27 = (f32[2,4,72,128]{3,2,1,0:T(8,128)S(1)}, f32[2,4,72,128]{3,2,1,0:T(8,128)S(1)}, u32[]{:S(2)}, u32[]{:S(2)}) collective-permute-start(f32[2,4,72,128]{3,2,1,0:T(8,128)S(1)} %get-tuple-element.95.other.field), channel_id=1, source_target_pairs={{0,8},{1,9},{2,10},{3,11},{4,12},{5,13},{6,14},{7,15},{8,0},{9,1},... | collective-permute-start | bytes 884744 | tf_op jit(solution)/shard_map/ppermute | solution.py:332
  60.1 8.9 %collective-permute-start.23 = (f32[2,4,72,128]{3,2,1,0:T(8,128)S(1)}, f32[2,4,72,128]{3,2,1,0:T(8,128)S(1)}, u32[]{:S(2)}, u32[]{:S(2)}) collective-permute-start(f32[2,4,72,128]{3,2,1,0:T(8,128)S(1)} %get-tuple-element.94.field.other), channel_id=1, source_target_pairs={{0,1},{1,0},{2,8},{3,9},{4,10},{5,11},{6,12},{7,13},{8,2},{9,3},{1... | collective-permute-start | bytes 884744 | tf_op jit(solution)/shard_map/ppermute | solution.py:332
  65.7 5.6 %collective-permute-start.28 = (f32[4,64,128]{2,1,0:T(8,128)S(1)}, f32[4,64,128]{2,1,0:T(8,128)S(1)}, u32[]{:S(2)}, u32[]{:S(2)}) collective-permute-start(f32[4,64,128]{2,1,0:T(8,128)S(1)} %get-tuple-element.99), channel_id=1, source_target_pairs={{0,0},{1,8},{2,2},{3,10},{4,4},{5,12},{6,6},{7,14},{8,1},{9,9},{10... | collective-permute-start | bytes 393224 | tf_op jit(solution)/shard_map/ppermute | solution.py:332
  66.4 6.8 %collective-permute-start.29 = (f32[4,64,128]{2,1,0:T(8,128)S(1)}, f32[4,64,128]{2,1,0:T(8,128)S(1)}, u32[]{:S(2)}, u32[]{:S(2)}) collective-permute-start(f32[4,64,128]{2,1,0:T(8,128)S(1)} %get-tuple-element.100), channel_id=1, source_target_pairs={{0,8},{1,0},{2,10},{3,2},{4,12},{5,4},{6,14},{7,6},{8,9},{9,1},{10... | collective-permute-start | bytes 393224 | tf_op jit(solution)/shard_map/ppermute | solution.py:332
  70.1 7.2 %collective-permute-start.26 = (f32[4,64,128]{2,1,0:T(8,128)S(1)}, f32[4,64,128]{2,1,0:T(8,128)S(1)}, u32[]{:S(2)}, u32[]{:S(2)}) collective-permute-start(f32[4,64,128]{2,1,0:T(8,128)S(1)} %get-tuple-element.98), channel_id=1, source_target_pairs={{0,8},{1,0},{2,10},{3,2},{4,12},{5,4},{6,14},{7,6},{8,9},{9,1},{10... | collective-permute-start | bytes 393224 | tf_op jit(solution)/shard_map/ppermute | solution.py:332
  (8 other events, 26.9 us)
where the time goes:
time: 78.3 us; the launch traced here: 78.1 us
  waiting for transfers between devices  37 us (47%)
  starting transfers between devices  31.8 us (41%)
  Pallas kernels  7.47 us (10%)
  local copies, waits for them, and re-layouts  1.41 us (2%)
    ppermute x30, waiting for transfers between devices, move(): return lax.ppermute(value, ('tm', 'space'), moves[name])  37 us
    ppermute x30, starting transfers between devices, move(): return lax.ppermute(value, ('tm', 'space'), moves[name])  31.8 us
    pallas_call x19, Pallas kernels, call(): pl.pallas_call(body, in_specs=specs, out_specs=[spec for spec, _ in outs]...  7.47 us
  transfers between devices with their start and end apart: 30, of which 13 were waited for; matrix products, arithmetic and copies ran while one was open for 0% of the time, Pallas kernels for 7%

commit v1 on v0

--- a/solution.py
+++ b/solution.py
@@ -12,6 +12,7 @@
 SUB = 8
 
 VMEM = pl.BlockSpec(memory_space=pltpu.VMEM)
+SMEM = pl.BlockSpec(memory_space=pltpu.SMEM)
 HBM = pl.BlockSpec(memory_space=pltpu.HBM)
 F32 = jnp.float32
 
@@ -109,13 +110,15 @@
 CONTINUES, INSIDE, LEFT = range(3)
 
 
-def table_of(matrix, weights):
+def table_kernel(matrix, weights, table):
     tm, space = lax.axis_index("tm"), lax.axis_index("space")
-    depth, x = space // 2, space % 2
     edge = jnp.where(tm % 2 == 0, 0, lax.axis_size("space") // 2 - 1)
-    masks = jnp.stack([tm // 2 != 0, depth != edge, x == 0]).astype(F32)
-    flat = jnp.concatenate([matrix.reshape(-1), weights, masks])
-    return jnp.broadcast_to(flat[:, None, None], (flat.shape[0], SUB, 128))
+    sections = weights.shape[0]
+    flat = [matrix[s, r] for s in range(sections) for r in range(sections)]
+    flat += [weights[r] for r in range(sections)]
+    flat += [jnp.where(mask, 1.0, 0.0) for mask in (tm // 2 != 0, space // 2 != edge, space % 2 == 0)]
+    for index, value in enumerate(flat):
+        table[index] = jnp.full(table.shape[1:], value, F32)
 
 
 def order_kernel(table, first, second, outer, inner, ends):
@@ -345,7 +348,8 @@
 
     states = pack((state,))
     given = pack((source, diffusion, reaction, start_field))
-    table = table_of(matrix, weights)
+    given_parameters = [(SMEM, matrix), (SMEM, weights)]
+    (table,) = call(table_kernel, given_parameters, within((sections * (sections + 1) + 3, SUB, 128)))
     outer, inner, ends = call(order_kernel, within(table, *states), within(pair, pair, double))
     kept = call(scale_kernel, within(table, *given), within(pair, (3, rows, nz), plane, plane) * 2)
     sources, coefs, fines, coarses = zip(kept[:4], kept[4:])

time: 78.3 us -> 78.2 us (level)
  local copies, waits for them, and re-layouts: 1.41 us -> 0.01 us
  waiting for transfers between devices: 37 us -> 37.9 us
    unnamed x4, local copies, waits for them, and re-layouts: 1.25 us -> 0.01 us
    ppermute x30, waiting for transfers between devices: 37 us -> 37.9 us  [move(): return lax.ppermute(value, ('tm', 'space'), moves[name])]
    pallas_call x19 -> x20, Pallas kernels: 7.47 us -> 7.93 us  [call(): pl.pallas_call(body, in_specs=specs, out_specs=[spec for spec, _ in outs]...]
where the time goes in v1:
time: 78.2 us; the launch traced here: 78 us
  waiting for transfers between devices  37.9 us (48%)
  starting transfers between devices  31.9 us (41%)
  Pallas kernels  7.93 us (10%)
    ppermute x30, waiting for transfers between devices, move(): return lax.ppermute(value, ('tm', 'space'), moves[name])  37.9 us
    ppermute x30, starting transfers between devices, move(): return lax.ppermute(value, ('tm', 'space'), moves[name])  31.9 us
    pallas_call x20, Pallas kernels, call(): pl.pallas_call(body, in_specs=specs, out_specs=[spec for spec, _ in outs]...  7.93 us
  transfers between devices with their start and end apart: 30, of which 13 were waited for; matrix products, arithmetic and copies ran while one was open for 0% of the time, Pallas kernels for 7%

profile of v1, /device:TPU:0, one launch (start us, length us, event | category | flops | bytes accessed | tf_op | source)
XLA Modules:
  0.0 78.0 jit_solution(5346762226401156327)
XLA Ops:
  1.9 4.2 %collective-permute-start.1 = (f32[2,4,72,128]{3,2,1,0:T(8,128)S(1)}, f32[2,4,72,128]{3,2,1,0:T(8,128)S(1)}, u32[]{:S(2)}, u32[]{:S(2)}) collective-permute-start(f32[2,4,72,128]{3,2,1,0:T(8,128)S(1)} %get-tuple-element.54), channel_id=1, source_target_pairs={{0,1},{1,9},{2,3},{3,11},{4,5},{5,13},{6,7},{7,15},{8,0},{9,8},{10... | collective-permute-start | bytes 884744 | tf_op jit(solution)/shard_map/ppermute | solution.py:335
  8.7 4.7 %collective-permute-done.1.second = f32[2,4,72,128]{3,2,1,0:T(8,128)S(1)} collective-permute-done((f32[2,4,72,128]{3,2,1,0:T(8,128)S(1)}, f32[2,4,72,128]{3,2,1,0:T(8,128)S(1)}, u32[]{:S(2)}, u32[]{:S(2)}) %collective-permute-start.1) | collective-permute-done | bytes 294944 | tf_op jit(solution)/shard_map/ppermute | solution.py:335
  14.8 1.5 %collective-permute-start.2 = (f32[2,4,72,128]{3,2,1,0:T(8,128)S(1)}, f32[2,4,72,128]{3,2,1,0:T(8,128)S(1)}, u32[]{:S(2)}, u32[]{:S(2)}) collective-permute-start(f32[2,4,72,128]{3,2,1,0:T(8,128)S(1)} %get-tuple-element.55.other.field), channel_id=1, source_target_pairs={{0,16},{1,17},{2,8},{3,9},{4,10},{5,11},{6,12},{7,13},{8,2},{9,3},... | collective-permute-start | bytes 884744 | tf_op jit(solution)/shard_map/ppermute | solution.py:335
  16.8 4.7 %collective-permute-done.5.second = f32[2,7,72,128]{3,2,1,0:T(8,128)S(1)} collective-permute-done((f32[2,7,72,128]{3,2,1,0:T(8,128)S(1)}, f32[2,7,72,128]{3,2,1,0:T(8,128)S(1)}, u32[]{:S(2)}, u32[]{:S(2)}) %collective-permute-start.5) | collective-permute-done | bytes 516128 | tf_op jit(solution)/shard_map/ppermute | solution.py:335
  23.8 1.4 %collective-permute-start.7 = (f32[2,4,72,128]{3,2,1,0:T(8,128)S(1)}, f32[2,4,72,128]{3,2,1,0:T(8,128)S(1)}, u32[]{:S(2)}, u32[]{:S(2)}) collective-permute-start(f32[2,4,72,128]{3,2,1,0:T(8,128)S(1)} %get-tuple-element.67.other.field), channel_id=1, source_target_pairs={{0,1},{1,0},{2,8},{3,9},{4,10},{5,11},{6,12},{7,13},{8,2},{9,3},{1... | collective-permute-start | bytes 884744 | tf_op jit(solution)/shard_map/ppermute | solution.py:335
  25.3 1.5 %collective-permute-start.8 = (f32[2,72,128]{2,1,0:T(8,128)S(1)}, f32[2,72,128]{2,1,0:T(8,128)S(1)}, u32[]{:S(2)}, u32[]{:S(2)}) collective-permute-start(f32[2,72,128]{2,1,0:T(8,128)S(1)} %get-tuple-element.69), channel_id=1, source_target_pairs={{0,16},{1,17},{2,18},{3,19},{4,20},{5,21},{6,22},{7,23},{8,24},{9,... | collective-permute-start | bytes 221192 | tf_op jit(solution)/shard_map/ppermute | solution.py:335
  26.8 2.8 %collective-permute-done.8.arrived = f32[2,72,128]{2,1,0:T(8,128)S(1)} collective-permute-done((f32[2,72,128]{2,1,0:T(8,128)S(1)}, f32[2,72,128]{2,1,0:T(8,128)S(1)}, u32[]{:S(2)}, u32[]{:S(2)}) %collective-permute-start.8) | collective-permute-done | bytes 73760 | tf_op jit(solution)/shard_map/ppermute | solution.py:335
  30.9 1.4 %collective-permute-start.10 = (f32[4,72,128]{2,1,0:T(8,128)S(1)}, f32[4,72,128]{2,1,0:T(8,128)S(1)}, u32[]{:S(2)}, u32[]{:S(2)}) collective-permute-start(f32[4,72,128]{2,1,0:T(8,128)S(1)} %get-tuple-element.73), channel_id=1, source_target_pairs={{0,1},{1,0},{2,8},{3,9},{4,10},{5,11},{6,12},{7,13},{8,2},{9,3},{1... | collective-permute-start | bytes 442376 | tf_op jit(solution)/shard_map/ppermute | solution.py:335
  32.4 1.5 %collective-permute-start.11 = (f32[2,72,128]{2,1,0:T(8,128)S(1)}, f32[2,72,128]{2,1,0:T(8,128)S(1)}, u32[]{:S(2)}, u32[]{:S(2)}) collective-permute-start(f32[2,72,128]{2,1,0:T(8,128)S(1)} %get-tuple-element.74), channel_id=1, source_target_pairs={{0,16},{1,17},{2,18},{3,19},{4,20},{5,21},{6,22},{7,23},{8,24},{9,... | collective-permute-start | bytes 221192 | tf_op jit(solution)/shard_map/ppermute | solution.py:335
  33.9 2.8 %collective-permute-done.11.arrived = f32[2,72,128]{2,1,0:T(8,128)S(1)} collective-permute-done((f32[2,72,128]{2,1,0:T(8,128)S(1)}, f32[2,72,128]{2,1,0:T(8,128)S(1)}, u32[]{:S(2)}, u32[]{:S(2)}) %collective-permute-start.11) | collective-permute-done | bytes 73760 | tf_op jit(solution)/shard_map/ppermute | solution.py:335
  38.2 1.5 %collective-permute-start.14 = (f32[2,72,128]{2,1,0:T(8,128)S(1)}, f32[2,72,128]{2,1,0:T(8,128)S(1)}, u32[]{:S(2)}, u32[]{:S(2)}) collective-permute-start(f32[2,72,128]{2,1,0:T(8,128)S(1)} %get-tuple-element.80), channel_id=1, source_target_pairs={{0,16},{1,17},{2,18},{3,19},{4,20},{5,21},{6,22},{7,23},{8,24},{9,... | collective-permute-start | bytes 221192 | tf_op jit(solution)/shard_map/ppermute | solution.py:335
  39.7 2.8 %collective-permute-done.14.arrived = f32[2,72,128]{2,1,0:T(8,128)S(1)} collective-permute-done((f32[2,72,128]{2,1,0:T(8,128)S(1)}, f32[2,72,128]{2,1,0:T(8,128)S(1)}, u32[]{:S(2)}, u32[]{:S(2)}) %collective-permute-start.14) | collective-permute-done | bytes 73760 | tf_op jit(solution)/shard_map/ppermute | solution.py:335
  43.0 1.6 %collective-permute-start.17 = (f32[2,72,128]{2,1,0:T(8,128)S(1)}, f32[2,72,128]{2,1,0:T(8,128)S(1)}, u32[]{:S(2)}, u32[]{:S(2)}) collective-permute-start(f32[2,72,128]{2,1,0:T(8,128)S(1)} %get-tuple-element.86), channel_id=1, source_target_pairs={{0,16},{1,17},{2,18},{3,19},{4,20},{5,21},{6,22},{7,23},{8,24},{9,... | collective-permute-start | bytes 221192 | tf_op jit(solution)/shard_map/ppermute | solution.py:335
  44.6 3.1 %collective-permute-done.17.arrived = f32[2,72,128]{2,1,0:T(8,128)S(1)} collective-permute-done((f32[2,72,128]{2,1,0:T(8,128)S(1)}, f32[2,72,128]{2,1,0:T(8,128)S(1)}, u32[]{:S(2)}, u32[]{:S(2)}) %collective-permute-start.17) | collective-permute-done | bytes 73760 | tf_op jit(solution)/shard_map/ppermute | solution.py:335
  48.0 1.5 %collective-permute-start.16 = (f32[4,72,128]{2,1,0:T(8,128)S(1)}, f32[4,72,128]{2,1,0:T(8,128)S(1)}, u32[]{:S(2)}, u32[]{:S(2)}) collective-permute-start(f32[4,72,128]{2,1,0:T(8,128)S(1)} %get-tuple-element.84.other.field), channel_id=1, source_target_pairs={{0,1},{1,0},{2,8},{3,9},{4,10},{5,11},{6,12},{7,13},{8,2},{9,3},{1... | collective-permute-start | bytes 442376 | tf_op jit(solution)/shard_map/ppermute | solution.py:335
  50.1 3.1 %collective-permute-done.16.halo = f32[4,72,128]{2,1,0:T(8,128)S(1)} collective-permute-done((f32[4,72,128]{2,1,0:T(8,128)S(1)}, f32[4,72,128]{2,1,0:T(8,128)S(1)}, u32[]{:S(2)}, u32[]{:S(2)}) %collective-permute-start.16) | collective-permute-done | bytes 147488 | tf_op jit(solution)/shard_map/ppermute | solution.py:335
  53.4 1.5 %collective-permute-start.19 = (f32[4,72,128]{2,1,0:T(8,128)S(1)}, f32[4,72,128]{2,1,0:T(8,128)S(1)}, u32[]{:S(2)}, u32[]{:S(2)}) collective-permute-start(f32[4,72,128]{2,1,0:T(8,128)S(1)} %get-tuple-element.90), channel_id=1, source_target_pairs={{0,1},{1,0},{2,8},{3,9},{4,10},{5,11},{6,12},{7,13},{8,2},{9,3},{1... | collective-permute-start | bytes 442376 | tf_op jit(solution)/shard_map/ppermute | solution.py:335
  54.9 1.5 %collective-permute-start.20 = (f32[2,72,128]{2,1,0:T(8,128)S(1)}, f32[2,72,128]{2,1,0:T(8,128)S(1)}, u32[]{:S(2)}, u32[]{:S(2)}) collective-permute-start(f32[2,72,128]{2,1,0:T(8,128)S(1)} %get-tuple-element.91), channel_id=1, source_target_pairs={{0,16},{1,17},{2,18},{3,19},{4,20},{5,21},{6,22},{7,23},{8,24},{9,... | collective-permute-start | bytes 221192 | tf_op jit(solution)/shard_map/ppermute | solution.py:335
  56.4 2.8 %collective-permute-done.20.arrived = f32[2,72,128]{2,1,0:T(8,128)S(1)} collective-permute-done((f32[2,72,128]{2,1,0:T(8,128)S(1)}, f32[2,72,128]{2,1,0:T(8,128)S(1)}, u32[]{:S(2)}, u32[]{:S(2)}) %collective-permute-start.20) | collective-permute-done | bytes 73760 | tf_op jit(solution)/shard_map/ppermute | solution.py:335
  60.9 1.5 %collective-permute-start.24 = (f32[2,72,128]{2,1,0:T(8,128)S(1)}, f32[2,72,128]{2,1,0:T(8,128)S(1)}, u32[]{:S(2)}, u32[]{:S(2)}) collective-permute-start(f32[2,72,128]{2,1,0:T(8,128)S(1)} %get-tuple-element.96), channel_id=1, source_target_pairs={{0,16},{1,17},{2,18},{3,19},{4,20},{5,21},{6,22},{7,23},{8,24},{9,... | collective-permute-start | bytes 221192 | tf_op jit(solution)/shard_map/ppermute | solution.py:335
  62.4 2.8 %collective-permute-done.24.arrived = f32[2,72,128]{2,1,0:T(8,128)S(1)} collective-permute-done((f32[2,72,128]{2,1,0:T(8,128)S(1)}, f32[2,72,128]{2,1,0:T(8,128)S(1)}, u32[]{:S(2)}, u32[]{:S(2)}) %collective-permute-start.24) | collective-permute-done | bytes 73760 | tf_op jit(solution)/shard_map/ppermute | solution.py:335
  66.3 2.6 %collective-permute-start.29 = (f32[4,64,128]{2,1,0:T(8,128)S(1)}, f32[4,64,128]{2,1,0:T(8,128)S(1)}, u32[]{:S(2)}, u32[]{:S(2)}) collective-permute-start(f32[4,64,128]{2,1,0:T(8,128)S(1)} %get-tuple-element.100), channel_id=1, source_target_pairs={{0,8},{1,0},{2,10},{3,2},{4,12},{5,4},{6,14},{7,6},{8,9},{9,1},{10... | collective-permute-start | bytes 393224 | tf_op jit(solution)/shard_map/ppermute | solution.py:335
  71.2 1.8 %collective-permute-done.29.second_inner = f32[4,64,128]{2,1,0:T(8,128)S(1)} collective-permute-done((f32[4,64,128]{2,1,0:T(8,128)S(1)}, f32[4,64,128]{2,1,0:T(8,128)S(1)}, u32[]{:S(2)}, u32[]{:S(2)}) %collective-permute-start.29) | collective-permute-done | bytes 131104 | tf_op jit(solution)/shard_map/ppermute | solution.py:335
  73.1 4.1 %collective-permute-done.26.second_outer = f32[4,64,128]{2,1,0:T(8,128)S(1)} collective-permute-done((f32[4,64,128]{2,1,0:T(8,128)S(1)}, f32[4,64,128]{2,1,0:T(8,128)S(1)}, u32[]{:S(2)}, u32[]{:S(2)}) %collective-permute-start.26) | collective-permute-done | bytes 131104 | tf_op jit(solution)/shard_map/ppermute | solution.py:335
  (60 shorter events, 18.5 us)
Async XLA Ops:
  1.2 7.6 %collective-permute-start = (f32[2,4,72,128]{3,2,1,0:T(8,128)S(1)}, f32[2,4,72,128]{3,2,1,0:T(8,128)S(1)}, u32[]{:S(2)}, u32[]{:S(2)}) collective-permute-start(f32[2,4,72,128]{3,2,1,0:T(8,128)S(1)} %get-tuple-element.53), channel_id=1, source_target_pairs={{0,0},{1,8},{2,2},{3,10},{4,4},{5,12},{6,6},{7,14},{8,1},{9,9},{10... | collective-permute-start | bytes 884744 | tf_op jit(solution)/shard_map/ppermute | solution.py:335
  1.9 11.6 %collective-permute-start.1 = (f32[2,4,72,128]{3,2,1,0:T(8,128)S(1)}, f32[2,4,72,128]{3,2,1,0:T(8,128)S(1)}, u32[]{:S(2)}, u32[]{:S(2)}) collective-permute-start(f32[2,4,72,128]{3,2,1,0:T(8,128)S(1)} %get-tuple-element.54), channel_id=1, source_target_pairs={{0,1},{1,9},{2,3},{3,11},{4,5},{5,13},{6,7},{7,15},{8,0},{9,8},{10... | collective-permute-start | bytes 884744 | tf_op jit(solution)/shard_map/ppermute | solution.py:335
  7.4 14.2 %collective-permute-start.5 = (f32[2,7,72,128]{3,2,1,0:T(8,128)S(1)}, f32[2,7,72,128]{3,2,1,0:T(8,128)S(1)}, u32[]{:S(2)}, u32[]{:S(2)}) collective-permute-start(f32[2,7,72,128]{3,2,1,0:T(8,128)S(1)} %get-tuple-element.59), channel_id=1, source_target_pairs={{0,1},{1,9},{2,3},{3,11},{4,5},{5,13},{6,7},{7,15},{8,0},{9,8},{10... | collective-permute-start | bytes 1548296 | tf_op jit(solution)/shard_map/ppermute | solution.py:335
  7.4 9.4 %collective-permute-start.4 = (f32[2,4,72,128]{3,2,1,0:T(8,128)S(1)}, f32[2,4,72,128]{3,2,1,0:T(8,128)S(1)}, u32[]{:S(2)}, u32[]{:S(2)}) collective-permute-start(f32[2,4,72,128]{3,2,1,0:T(8,128)S(1)} %get-tuple-element.58), channel_id=1, source_target_pairs={{0,0},{1,8},{2,2},{3,10},{4,4},{5,12},{6,6},{7,14},{8,1},{9,9},{10... | collective-permute-start | bytes 884744 | tf_op jit(solution)/shard_map/ppermute | solution.py:335
  13.5 9.6 %collective-permute-start.6 = (f32[2,4,72,128]{3,2,1,0:T(8,128)S(1)}, f32[2,4,72,128]{3,2,1,0:T(8,128)S(1)}, u32[]{:S(2)}, u32[]{:S(2)}) collective-permute-start(f32[2,4,72,128]{3,2,1,0:T(8,128)S(1)} %get-tuple-element.56.field.other), channel_id=1, source_target_pairs={{0,8},{1,9},{2,10},{3,11},{4,12},{5,13},{6,14},{7,15},{8,0},{9,1},... | collective-permute-start | bytes 884744 | tf_op jit(solution)/shard_map/ppermute | solution.py:335
  14.8 8.7 %collective-permute-start.2 = (f32[2,4,72,128]{3,2,1,0:T(8,128)S(1)}, f32[2,4,72,128]{3,2,1,0:T(8,128)S(1)}, u32[]{:S(2)}, u32[]{:S(2)}) collective-permute-start(f32[2,4,72,128]{3,2,1,0:T(8,128)S(1)} %get-tuple-element.55.other.field), channel_id=1, source_target_pairs={{0,16},{1,17},{2,8},{3,9},{4,10},{5,11},{6,12},{7,13},{8,2},{9,3},... | collective-permute-start | bytes 884744 | tf_op jit(solution)/shard_map/ppermute | solution.py:335
  16.3 6.8 %collective-permute-start.3 = (f32[2,72,128]{2,1,0:T(8,128)S(1)}, f32[2,72,128]{2,1,0:T(8,128)S(1)}, u32[]{:S(2)}, u32[]{:S(2)}) collective-permute-start(f32[2,72,128]{2,1,0:T(8,128)S(1)} %get-tuple-element.57), channel_id=1, source_target_pairs={{0,16},{1,17},{2,18},{3,19},{4,20},{5,21},{6,22},{7,23},{8,24},{9,... | collective-permute-start | bytes 221192 | tf_op jit(solution)/shard_map/ppermute | solution.py:335
  23.4 6.2 %collective-permute-start.9 = (f32[2,4,72,128]{3,2,1,0:T(8,128)S(1)}, f32[2,4,72,128]{3,2,1,0:T(8,128)S(1)}, u32[]{:S(2)}, u32[]{:S(2)}) collective-permute-start(f32[2,4,72,128]{3,2,1,0:T(8,128)S(1)} %get-tuple-element.68.field.other), channel_id=1, source_target_pairs={{0,8},{1,9},{2,10},{3,11},{4,12},{5,13},{6,14},{7,15},{8,0},{9,1},... | collective-permute-start | bytes 884744 | tf_op jit(solution)/shard_map/ppermute | solution.py:335
  23.8 6.8 %collective-permute-start.7 = (f32[2,4,72,128]{3,2,1,0:T(8,128)S(1)}, f32[2,4,72,128]{3,2,1,0:T(8,128)S(1)}, u32[]{:S(2)}, u32[]{:S(2)}) collective-permute-start(f32[2,4,72,128]{3,2,1,0:T(8,128)S(1)} %get-tuple-element.67.other.field), channel_id=1, source_target_pairs={{0,1},{1,0},{2,8},{3,9},{4,10},{5,11},{6,12},{7,13},{8,2},{9,3},{1... | collective-permute-start | bytes 884744 | tf_op jit(solution)/shard_map/ppermute | solution.py:335
  29.9 6.8 %collective-permute-start.12 = (f32[2,4,72,128]{3,2,1,0:T(8,128)S(1)}, f32[2,4,72,128]{3,2,1,0:T(8,128)S(1)}, u32[]{:S(2)}, u32[]{:S(2)}) collective-permute-start(f32[2,4,72,128]{3,2,1,0:T(8,128)S(1)} %get-tuple-element.72.field.other.refs_0_), channel_id=1, source_target_pairs={{0,8},{1,9},{2,10},{3,11},{4,12},{5,13},{6,14},{7,15},{8,0},{9,1},... | collective-permute-start | bytes 884744 | tf_op jit(solution)/shard_map/ppermute | solution.py:335
  30.9 6.2 %collective-permute-start.10 = (f32[4,72,128]{2,1,0:T(8,128)S(1)}, f32[4,72,128]{2,1,0:T(8,128)S(1)}, u32[]{:S(2)}, u32[]{:S(2)}) collective-permute-start(f32[4,72,128]{2,1,0:T(8,128)S(1)} %get-tuple-element.73), channel_id=1, source_target_pairs={{0,1},{1,0},{2,8},{3,9},{4,10},{5,11},{6,12},{7,13},{8,2},{9,3},{1... | collective-permute-start | bytes 442376 | tf_op jit(solution)/shard_map/ppermute | solution.py:335
  37.0 5.5 %collective-permute-start.15 = (f32[4,72,128]{2,1,0:T(8,128)S(1)}, f32[4,72,128]{2,1,0:T(8,128)S(1)}, u32[]{:S(2)}, u32[]{:S(2)}) collective-permute-start(f32[4,72,128]{2,1,0:T(8,128)S(1)} %get-tuple-element.79.field.other), channel_id=1, source_target_pairs={{0,8},{1,9},{2,10},{3,11},{4,12},{5,13},{6,14},{7,15},{8,0},{9,1},... | collective-permute-start | bytes 442376 | tf_op jit(solution)/shard_map/ppermute | solution.py:335
  37.4 5.4 %collective-permute-start.13 = (f32[4,72,128]{2,1,0:T(8,128)S(1)}, f32[4,72,128]{2,1,0:T(8,128)S(1)}, u32[]{:S(2)}, u32[]{:S(2)}) collective-permute-start(f32[4,72,128]{2,1,0:T(8,128)S(1)} %get-tuple-element.78.other.field), channel_id=1, source_target_pairs={{0,1},{1,0},{2,8},{3,9},{4,10},{5,11},{6,12},{7,13},{8,2},{9,3},{1... | collective-permute-start | bytes 442376 | tf_op jit(solution)/shard_map/ppermute | solution.py:335
  42.7 5.0 %collective-permute-start.18 = (f32[4,72,128]{2,1,0:T(8,128)S(1)}, f32[4,72,128]{2,1,0:T(8,128)S(1)}, u32[]{:S(2)}, u32[]{:S(2)}) collective-permute-start(f32[4,72,128]{2,1,0:T(8,128)S(1)} %get-tuple-element.85.field.other), channel_id=1, source_target_pairs={{0,8},{1,9},{2,10},{3,11},{4,12},{5,13},{6,14},{7,15},{8,0},{9,1},... | collective-permute-start | bytes 442376 | tf_op jit(solution)/shard_map/ppermute | solution.py:335
  43.0 4.7 %collective-permute-start.17 = (f32[2,72,128]{2,1,0:T(8,128)S(1)}, f32[2,72,128]{2,1,0:T(8,128)S(1)}, u32[]{:S(2)}, u32[]{:S(2)}) collective-permute-start(f32[2,72,128]{2,1,0:T(8,128)S(1)} %get-tuple-element.86), channel_id=1, source_target_pairs={{0,16},{1,17},{2,18},{3,19},{4,20},{5,21},{6,22},{7,23},{8,24},{9,... | collective-permute-start | bytes 221192 | tf_op jit(solution)/shard_map/ppermute | solution.py:335
  47.9 11.3 %collective-permute-start.21 = (f32[2,4,72,128]{3,2,1,0:T(8,128)S(1)}, f32[2,4,72,128]{3,2,1,0:T(8,128)S(1)}, u32[]{:S(2)}, u32[]{:S(2)}) collective-permute-start(f32[2,4,72,128]{3,2,1,0:T(8,128)S(1)} %get-tuple-element.89.field.other), channel_id=1, source_target_pairs={{0,8},{1,9},{2,10},{3,11},{4,12},{5,13},{6,14},{7,15},{8,0},{9,1},... | collective-permute-start | bytes 884744 | tf_op jit(solution)/shard_map/ppermute | solution.py:335
  48.0 5.2 %collective-permute-start.16 = (f32[4,72,128]{2,1,0:T(8,128)S(1)}, f32[4,72,128]{2,1,0:T(8,128)S(1)}, u32[]{:S(2)}, u32[]{:S(2)}) collective-permute-start(f32[4,72,128]{2,1,0:T(8,128)S(1)} %get-tuple-element.84.other.field), channel_id=1, source_target_pairs={{0,1},{1,0},{2,8},{3,9},{4,10},{5,11},{6,12},{7,13},{8,2},{9,3},{1... | collective-permute-start | bytes 442376 | tf_op jit(solution)/shard_map/ppermute | solution.py:335
  49.5 10.1 %collective-permute-start.22 = (f32[4,72,128]{2,1,0:T(8,128)S(1)}, f32[4,72,128]{2,1,0:T(8,128)S(1)}, u32[]{:S(2)}, u32[]{:S(2)}) collective-permute-start(f32[4,72,128]{2,1,0:T(8,128)S(1)} %get-tuple-element.93), channel_id=1, source_target_pairs={{0,1},{1,0},{2,8},{3,9},{4,10},{5,11},{6,12},{7,13},{8,2},{9,3},{1... | collective-permute-start | bytes 442376 | tf_op jit(solution)/shard_map/ppermute | solution.py:335
  53.4 6.2 %collective-permute-start.19 = (f32[4,72,128]{2,1,0:T(8,128)S(1)}, f32[4,72,128]{2,1,0:T(8,128)S(1)}, u32[]{:S(2)}, u32[]{:S(2)}) collective-permute-start(f32[4,72,128]{2,1,0:T(8,128)S(1)} %get-tuple-element.90), channel_id=1, source_target_pairs={{0,1},{1,0},{2,8},{3,9},{4,10},{5,11},{6,12},{7,13},{8,2},{9,3},{1... | collective-permute-start | bytes 442376 | tf_op jit(solution)/shard_map/ppermute | solution.py:335
  59.5 5.7 %collective-permute-start.27 = (f32[2,4,72,128]{3,2,1,0:T(8,128)S(1)}, f32[2,4,72,128]{3,2,1,0:T(8,128)S(1)}, u32[]{:S(2)}, u32[]{:S(2)}) collective-permute-start(f32[2,4,72,128]{3,2,1,0:T(8,128)S(1)} %get-tuple-element.95.other.field), channel_id=1, source_target_pairs={{0,8},{1,9},{2,10},{3,11},{4,12},{5,13},{6,14},{7,15},{8,0},{9,1},... | collective-permute-start | bytes 884744 | tf_op jit(solution)/shard_map/ppermute | solution.py:335
  60.0 8.9 %collective-permute-start.23 = (f32[2,4,72,128]{3,2,1,0:T(8,128)S(1)}, f32[2,4,72,128]{3,2,1,0:T(8,128)S(1)}, u32[]{:S(2)}, u32[]{:S(2)}) collective-permute-start(f32[2,4,72,128]{3,2,1,0:T(8,128)S(1)} %get-tuple-element.94.field.other), channel_id=1, source_target_pairs={{0,1},{1,0},{2,8},{3,9},{4,10},{5,11},{6,12},{7,13},{8,2},{9,3},{1... | collective-permute-start | bytes 884744 | tf_op jit(solution)/shard_map/ppermute | solution.py:335
  65.6 5.6 %collective-permute-start.28 = (f32[4,64,128]{2,1,0:T(8,128)S(1)}, f32[4,64,128]{2,1,0:T(8,128)S(1)}, u32[]{:S(2)}, u32[]{:S(2)}) collective-permute-start(f32[4,64,128]{2,1,0:T(8,128)S(1)} %get-tuple-element.99), channel_id=1, source_target_pairs={{0,0},{1,8},{2,2},{3,10},{4,4},{5,12},{6,6},{7,14},{8,1},{9,9},{10... | collective-permute-start | bytes 393224 | tf_op jit(solution)/shard_map/ppermute | solution.py:335
  66.3 6.8 %collective-permute-start.29 = (f32[4,64,128]{2,1,0:T(8,128)S(1)}, f32[4,64,128]{2,1,0:T(8,128)S(1)}, u32[]{:S(2)}, u32[]{:S(2)}) collective-permute-start(f32[4,64,128]{2,1,0:T(8,128)S(1)} %get-tuple-element.100), channel_id=1, source_target_pairs={{0,8},{1,0},{2,10},{3,2},{4,12},{5,4},{6,14},{7,6},{8,9},{9,1},{10... | collective-permute-start | bytes 393224 | tf_op jit(solution)/shard_map/ppermute | solution.py:335
  69.9 7.2 %collective-permute-start.26 = (f32[4,64,128]{2,1,0:T(8,128)S(1)}, f32[4,64,128]{2,1,0:T(8,128)S(1)}, u32[]{:S(2)}, u32[]{:S(2)}) collective-permute-start(f32[4,64,128]{2,1,0:T(8,128)S(1)} %get-tuple-element.98), channel_id=1, source_target_pairs={{0,8},{1,0},{2,10},{3,2},{4,12},{5,4},{6,14},{7,6},{8,9},{9,1},{10... | collective-permute-start | bytes 393224 | tf_op jit(solution)/shard_map/ppermute | solution.py:335
  (8 other events, 27.1 us)
